TPU v7x, 32 devices: a whole 2x2x4 slice. The times are simulated.
32 devices in a mesh: dom: 16 (over z, x, core), rep: 2 (over y).
Axes of the slice: x: 2, y: 2, z: 4, core: 2. Of those that a mesh axis runs over, the one named last changes fastest.
Arguments:
- features: bfloat16 [131072, 128], P('dom'), may hold values from -6 to 6
- partition_map: int32 [131072], replicated, may hold values from 0 to 131071, as said below
- seed_ids: int32 [2048], P(('dom', 'rep')), may hold values from 0 to 131071, as said below
- hop1_ids: int32 [2048, 15], P(('dom', 'rep')), may hold values from 0 to 131071, as said below
- hop2_ids: int32 [2048, 15, 10], P(('dom', 'rep')), may hold values from 0 to 131071, as said below
- labels: int32 [2048], P(('dom', 'rep')), may hold values from 0 to 171
- self_one: bfloat16 [128, 256], replicated, may hold values from -0.5 to 0.5
- neigh_one: bfloat16 [128, 256], replicated, may hold values from -0.5 to 0.5
- bias_one: float32 [256], replicated, may hold values from -3 to 3
- self_two: bfloat16 [256, 172], replicated, may hold values from -0.375 to 0.375
- neigh_two: bfloat16 [256, 172], replicated, may hold values from -0.375 to 0.375
- bias_two: float32 [172], replicated, may hold values from -2 to 112, as said below
Outputs:
- seed_loss: float32 [2048], P(('dom', 'rep'))
- grad_self_one: float32 [128, 256], replicated
- grad_neigh_one: float32 [128, 256], replicated
- grad_bias_one: float32 [256], replicated
- grad_self_two: float32 [256, 172], replicated
- grad_neigh_two: float32 [256, 172], replicated
- grad_bias_two: float32 [172], replicated
Inputs may be any that keep to these rules, and one draw needn't show every extreme that they name: A permutation of 0 to 131071: node v is stored at position p = partition_map[v], in partition p // 8192, row p % 8192. Rows below 256 of each partition hold hub nodes. `seed_ids`: node ids. `hop1_ids`: node ids. `hop2_ids`: take one device's 64 seeds (an aligned block of seeds) with all their hop-1 and hop-2 ids, 10624 ids with repeats counted, and map them through partition_map: at most 2428 positions fall in any one partition, and at most 332 fall in rows 256 and above of any one partition. Every device reaches both bounds. `bias_two`: class biases.
All inputs are finite; a program needn't handle non-finite values.
Results may differ from a plain program's by a relative error of at most 0.003.
Values may be sent and summed in bfloat16 or wider, within the bound.
A program may use at most 128 MiB of HBM per device.

v0:
```python
import jax
import jax.numpy as jnp
from jax import lax
from jax.sharding import PartitionSpec as P

HOT_DEV = 256


def activate(values):
    return jax.nn.gelu(values, approximate=True)


def sage_terms(
    seed_rows,
    hop_rows,
    far_rows,
    labels,
    self_one,
    neigh_one,
    bias_one,
    self_two,
    neigh_two,
    bias_two,
):
    seed_count = seed_rows.shape[0]
    fan_one = hop_rows.shape[0] // seed_count
    feat_width = seed_rows.shape[1]
    hidden = self_one.shape[1]
    seed_mean = jnp.mean(
        hop_rows.reshape(seed_count, fan_one, feat_width), axis=1, dtype=jnp.float32
    ).astype(jnp.bfloat16)
    far_mean = jnp.mean(far_rows, axis=1, dtype=jnp.float32).astype(jnp.bfloat16)
    pre_seed = (
        jnp.dot(seed_rows, self_one, preferred_element_type=jnp.float32)
        + jnp.dot(seed_mean, neigh_one, preferred_element_type=jnp.float32)
        + bias_one
    )
    pre_hop = (
        jnp.dot(hop_rows, self_one, preferred_element_type=jnp.float32)
        + jnp.dot(far_mean, neigh_one, preferred_element_type=jnp.float32)
        + bias_one
    )
    act_seed, back_seed = jax.vjp(activate, pre_seed)
    act_hop, back_hop = jax.vjp(activate, pre_hop)
    hid_seed = act_seed.astype(jnp.bfloat16)
    hid_hop = act_hop.astype(jnp.bfloat16)
    hop_mean = jnp.mean(
        hid_hop.reshape(seed_count, fan_one, hidden), axis=1, dtype=jnp.float32
    ).astype(jnp.bfloat16)
    logits = (
        jnp.dot(hid_seed, self_two, preferred_element_type=jnp.float32)
        + jnp.dot(hop_mean, neigh_two, preferred_element_type=jnp.float32)
        + bias_two
    )
    peak_value = jnp.max(logits, axis=1, keepdims=True)
    shifted = logits - peak_value
    log_total = jnp.log(jnp.sum(jnp.exp(shifted), axis=1, keepdims=True))
    log_probs = shifted - log_total
    class_iota = lax.broadcasted_iota(jnp.int32, logits.shape, 1)
    target = (labels[:, None] == class_iota).astype(jnp.float32)
    seed_loss = -jnp.sum(log_probs * target, axis=1)
    d_logits = ((jnp.exp(log_probs) - target) / seed_count).astype(jnp.bfloat16)
    grad_self_two = jnp.dot(hid_seed.T, d_logits, preferred_element_type=jnp.float32)
    grad_neigh_two = jnp.dot(hop_mean.T, d_logits, preferred_element_type=jnp.float32)
    grad_bias_two = jnp.sum(d_logits.astype(jnp.float32), axis=0)
    d_hid_seed = jnp.dot(d_logits, self_two.T, preferred_element_type=jnp.float32)
    d_hop_mean = jnp.dot(d_logits, neigh_two.T, preferred_element_type=jnp.float32)
    d_pre_seed = back_seed(d_hid_seed)[0].astype(jnp.bfloat16)
    spread = jnp.broadcast_to(
        (d_hop_mean / fan_one)[:, None, :], (seed_count, fan_one, hidden)
    ).reshape(seed_count * fan_one, hidden)
    d_pre_hop = back_hop(spread)[0].astype(jnp.bfloat16)
    grad_self_one = jnp.dot(seed_rows.T, d_pre_seed, preferred_element_type=jnp.float32) + jnp.dot(
        hop_rows.T, d_pre_hop, preferred_element_type=jnp.float32
    )
    grad_neigh_one = jnp.dot(seed_mean.T, d_pre_seed, preferred_element_type=jnp.float32) + jnp.dot(
        far_mean.T, d_pre_hop, preferred_element_type=jnp.float32
    )
    grad_bias_one = jnp.sum(d_pre_seed.astype(jnp.float32), axis=0) + jnp.sum(
        d_pre_hop.astype(jnp.float32), axis=0
    )
    return (
        seed_loss,
        (
            grad_self_one,
            grad_neigh_one,
            grad_bias_one,
            grad_self_two,
            grad_neigh_two,
            grad_bias_two,
        ),
    )


def bucket_slots(owners, chosen, part_count):
    columns = lax.broadcasted_iota(jnp.int32, (owners.shape[0], part_count), 1)
    member = ((owners[:, None] == columns) & chosen[:, None]).astype(jnp.int32)
    running = jnp.cumsum(member, axis=0)
    return jnp.sum(running * member, axis=1) - 1


def request_table(owners, slots, local_rows, part_count, capacity):
    target_slot = jnp.where(slots >= 0, slots, capacity)
    table = jnp.zeros((part_count, capacity), jnp.int32)
    return table.at[owners, target_slot].set(local_rows, mode="drop")


def shards(
    features,
    partition_map,
    seed_ids,
    hop1_ids,
    hop2_ids,
    labels,
    self_one,
    neigh_one,
    bias_one,
    self_two,
    neigh_two,
    bias_two,
):
    part_count = lax.axis_size("dom")
    seed_count = seed_ids.shape[0]
    fan_one = hop1_ids.shape[1]
    fan_two = hop2_ids.shape[2]
    node_rows = features.shape[0]
    feat_width = features.shape[1]
    tree_rows = 1 + fan_one + fan_one * fan_two
    seed_unit = seed_count // part_count
    cold_cap = tree_rows // 2 * seed_unit
    wanted = jnp.concatenate([seed_ids, hop1_ids.reshape(-1), hop2_ids.reshape(-1)])
    position = partition_map[wanted]
    owners = position // node_rows
    local_rows = position % node_rows
    is_cold = local_rows >= HOT_DEV
    slots = bucket_slots(owners, is_cold, part_count)
    request = request_table(owners, slots, local_rows, part_count, cold_cap)
    arrived = lax.all_to_all(request, "dom", split_axis=0, concat_axis=0, tiled=True)
    returned = lax.all_to_all(features[arrived], "dom", split_axis=0, concat_axis=0, tiled=True)
    hub_rows = lax.all_gather(features[:HOT_DEV], "dom", axis=0, tiled=True)
    from_far = returned[owners, jnp.maximum(slots, 0)]
    from_hub = hub_rows[owners * HOT_DEV + jnp.minimum(local_rows, HOT_DEV - 1)]
    fetched = jnp.where(is_cold[:, None], from_far, from_hub)
    seed_rows = fetched[:seed_count]
    hop_rows = fetched[seed_count : seed_count * (1 + fan_one)]
    far_rows = fetched[seed_count * (1 + fan_one) :].reshape(
        seed_count * fan_one, fan_two, feat_width
    )
    seed_loss, grads = sage_terms(
        seed_rows,
        hop_rows,
        far_rows,
        labels,
        self_one,
        neigh_one,
        bias_one,
        self_two,
        neigh_two,
        bias_two,
    )
    grad_self_one, grad_neigh_one, grad_bias_one, grad_self_two, grad_neigh_two, grad_bias_two = (
        grads
    )
    summed = lax.psum(
        (
            grad_self_one,
            grad_neigh_one,
            grad_bias_one,
            grad_self_two,
            grad_neigh_two,
            grad_bias_two,
        ),
        ("dom", "rep"),
    )
    return (seed_loss, summed[0], summed[1], summed[2], summed[3], summed[4], summed[5])


def solution(mesh):
    return jax.shard_map(
        shards,
        mesh=mesh,
        in_specs=(
            P("dom", None),
            P(),
            P(("dom", "rep")),
            P(("dom", "rep"), None),
            P(("dom", "rep"), None, None),
            P(("dom", "rep")),
            P(),
            P(),
            P(),
            P(),
            P(),
            P(),
        ),
        out_specs=(P(("dom", "rep")), P(), P(), P(), P(), P(), P()),
        check_vma=False,
    )
```

profile of v0, /device:TPU:0, one launch (start us, length us, event | category | flops | bytes accessed | tf_op | source)
XLA Modules:
  0.0 499.8 jit_solution(7547511234379188678)
XLA Ops:
  7.2 1.2 copy.25
  8.4 0.3 concatenate.36
  8.7 0.8 copy.24
  9.7 0.8 concatenate.37
  10.6 54.9 %gather_fusion = s32[10624]{0:T(1024)S(1)} fusion(s32[131072]{0:T(1024)S(1)} %copy-done, s32[11264]{0:T(1024)S(1)} %pad_clamp_fusion.1), kind=kCustom, calls=%fused_computation | custom fusion | bytes 127488 | tf_op jit(solution)/shard_map/gather | solution.py:132
  65.6 0.9 fusion.11
  66.6 9.2 %reduce-window.6 = s32[16,83,128]{2,1,0:T(8,128)S(1)} reduce-window(s32[16,83,128]{2,1,0:T(8,128)} %fusion.11, s32[]{:T(128)} %constant.33.clone.1), window={size=1x1x128 pad=0_0x0_0x127_0}, to_apply=%region_0.1 | reduce-window | flops 21587968 | bytes 1359876 | tf_op jit(solution)/shard_map/reduce-window
  75.8 0.6 slice_reduce_fusion
  77.1 0.8 or_reduce_fusion
  78.3 50.0 %scatter_custom_fusion = s32[5312]{0:T(1024)S(1)} fusion(s32[10624]{0:T(1024)S(1)} %broadcast_select_fusion.1, s32[10624]{0:T(1024)S(1)} %get-tuple-element.22, s32[]{:T(128)} %constant.33.clone.1), kind=kCustom, calls=%fused_computation.111 | custom fusion | bytes 21252
  128.4 13.8 %all_to_all.17 = s32[16,1,332]{2,1,0:T(1,128)S(1)} all-to-all(s32[16,1,332]{2,1,0:T(1,128)S(1)} %all_to_all.11), channel_id=1, replica_groups=mesh['dom'=16,'rep'=2] {'dom'}, dimensions={0} | all-to-all | bytes 42496 | tf_op jit(solution)/shard_map/all_to_all | solution.py:138
  142.4 11.6 %gather_fusion.1 = bf16[5312,128]{1,0:T(8,128)(2,1)} fusion(bf16[8192,128]{1,0:T(8,128)(2,1)S(1)} %copy-done.1, s32[6144]{0:T(1024)S(1)} %pad_clamp_fusion.2), kind=kCustom, calls=%fused_computation.1 | custom fusion | bytes 2740992 | tf_op jit(solution)/shard_map/gather | solution.py:139
  154.0 2.3 reshape.364
  156.3 4.4 all-to-all-start.1
  160.8 0.6 slice.20
  161.7 47.2 %all-gather.2.cloned.1.call-done = bf16[4096,128]{1,0:T(8,128)(2,1)} async-done(((bf16[256,128]{1,0:T(8,128)(2,1)}), bf16[4096,128]{1,0:T(8,128)(2,1)}) %all-gather.2.cloned.1.call-update) | async-done | bytes 1048592 | tf_op jit(solution)/shard_map/all_gather | solution.py:140
  208.9 21.8 %gather_fusion.3 = bf16[10624,128]{1,0:T(8,128)(2,1)} fusion(bf16[4096,128]{1,0:T(8,128)(2,1)} %all-gather.2.cloned.1.call-done, s32[11264]{0:T(1024)S(1)} %pad_clamp_fusion), kind=kCustom, calls=%fused_computation.3 | custom fusion | bytes 5481984 | tf_op jit(solution)/shard_map/gather | solution.py:142
  230.7 1.7 copy.26
  232.4 76.5 %gather_fusion.2 = bf16[10624,128]{1,0:T(8,128)(2,1)} fusion(bf16[16,332,128]{2,0,1:T(8,128)(2,1)S(1)} %copy.26, s32[10624]{0:T(1024)S(1)} %get-tuple-element.19), kind=kCustom, calls=%fused_computation.2 | custom fusion | bytes 5524480 | tf_op jit(solution)/shard_map/gather | solution.py:141
  309.0 7.6 %broadcast_select_fusion = bf16[10624,128]{1,0:T(8,128)(2,1)S(1)} fusion(bf16[10624,128]{1,0:T(8,128)(2,1)} %gather_fusion.2, bf16[10624,128]{1,0:T(8,128)(2,1)} %gather_fusion.3, pred[10624]{0:T(1024)(128)(4,1)S(1)} %get-tuple-element.21), kind=kLoop, calls=%fused_computation.5 | loop fusion | flops 1359872 | bytes 8169856 | tf_op jit(solution)/shard_map/jit(_where)/select_n | solution.py:143
  316.5 2.4 slice_convert_fusion
  318.9 0.8 slice_convert_fusion.1
  319.7 1.3 fusion.17
  321.0 0.8 fusion.39
  321.8 6.6 %reshape.353 = f32[960,10,128]{2,1,0:T(8,128)} reshape(f32[9600,128]{1,0:T(8,128)} %slice_convert_fusion) | data formatting | bytes 9830400 | tf_op jit(solution)/shard_map/convert_element_type | solution.py:32
  328.4 5.3 %reduce_sum.83 = f32[960,128]{1,0:T(8,128)} reduce(f32[960,10,128]{2,1,0:T(8,128)} %reshape.353, f32[]{:T(128)} %constant.78.clone.1), dimensions={1}, to_apply=%region_5.6 | reduce | flops 1105920 | bytes 5406724 | tf_op jit(solution)/shard_map/reduce_sum | solution.py:32
  333.7 3.2 fusion.15
  336.9 2.3 reshape.354
  339.2 1.4 reduce_sum.84
  340.7 1.9 reshape.352
  342.5 1.1 reduce_sum.82
  343.6 1.0 fusion.2
  344.6 1.1 fusion.52
  346.5 1.1 convert_reduce_fusion.2
  347.6 0.9 fusion.41
  348.5 0.9 fusion.51
  349.8 1.1 broadcast_in_dim.13
  350.9 2.3 reshape.346
  353.2 2.3 convert_reduce_fusion
  355.4 0.9 convolution_add_fusion.1
  356.4 0.9 convolution_add_fusion.2
  357.3 0.5 neg.3
  357.8 38.8 %all-reduce = (f32[256]{0:T(256)}, f32[172]{0:T(256)}) all-reduce(f32[256]{0:T(256)S(1)} %add.216, f32[172]{0:T(256)S(1)} %get-tuple-element.13), channel_id=1, replica_groups=mesh['dom'=16,'rep'=2] {'dom','rep'}, use_global_device_ids=true, to_apply=%region_14.15 | all-reduce | flops 428 | bytes 3424 | tf_op jit(solution)/shard_map/psum | solution.py:164
  396.6 90.0 %all-reduce.4.cloned.1.call-done = (f32[128,256]{1,0:T(8,128)}, f32[128,256]{1,0:T(8,128)}, f32[256,172]{0,1:T(8,128)}, f32[256,172]{0,1:T(8,128)}) async-done(((f32[128,256]{1,0:T(8,128)}, f32[128,256]{1,0:T(8,128)}, f32[256,172]{0,1:T(8,128)}, f32[256,172]{0,1:T(8,128)}), (f32[128,256]{1,0:T(8,128)}, f32[128,256]{1,0:T(8,128)}, f32[256,172]{0,1:T(8,128)}, ...) | async-done | bytes 614416 | tf_op jit(solution)/shard_map/psum | solution.py:164
  486.6 1.6 copy.33
  488.2 1.6 copy.34
  489.8 1.6 copy.35
  491.4 1.6 copy.36
  (54 shorter events, 3.5 us)
Async XLA Ops:
  7.2 3.4 copy-start
  65.6 12.3 %copy-start.10 = (s32[2]{0:T(128)S(1)}, s32[2]{0:T(128)}, u32[]{:S(2)}) copy-start(s32[2]{0:T(128)} %constant.89) | copy-start | bytes 28
  65.6 12.5 %copy-start.9 = (s32[2]{0:T(128)S(1)}, s32[2]{0:T(128)}, u32[]{:S(2)}) copy-start(s32[2]{0:T(128)} %constant.92) | copy-start | bytes 28
  66.6 75.8 %copy-start.1 = (bf16[8192,128]{1,0:T(8,128)(2,1)S(1)}, bf16[8192,128]{1,0:T(8,128)(2,1)}, u32[]{:S(2)}) copy-start(bf16[8192,128]{1,0:T(8,128)(2,1)} %param.12) | copy-start | bytes 6291460
  156.3 74.4 %all-to-all-start.1 = ((bf16[16,332,128]{2,1,0:T(8,128)(2,1)}), bf16[16,332,128]{2,1,0:T(8,128)(2,1)}, u32[]{:S(2)}, u32[]{:S(2)}) async-start(bf16[16,332,128]{2,1,0:T(8,128)(2,1)} %reshape.364), calls=%async_computation.1 | async-start | bytes 2752512 | tf_op jit(solution)/shard_map/all_to_all | solution.py:139
  160.7 48.2 %all-gather.2.cloned.1.call-start = ((), (), s32[]{:S(2)}) async-start(), calls=%async_computation.2 | async-start | bytes 1114112 | tf_op jit(solution)/shard_map/all_gather | solution.py:140
  161.5 325.2 %all-reduce.4.cloned.1.call-start = ((), (), s32[]{:S(2)}) async-start(), calls=%async_computation.3 | async-start | bytes 1245184 | tf_op jit(solution)/shard_map/psum | solution.py:164
  316.5 3.2 copy-start.5
  328.4 5.3 %copy-start.4 = (bf16[128,256]{1,0:T(8,128)(2,1)S(1)}, bf16[128,256]{1,0:T(8,128)(2,1)}, u32[]{:S(2)}) copy-start(bf16[128,256]{1,0:T(8,128)(2,1)} %param.19) | copy-start | bytes 196612
  328.4 5.3 %copy-start.6 = (f32[256]{0:T(256)S(1)}, f32[256]{0:T(256)}, u32[]{:S(2)}) copy-start(f32[256]{0:T(256)} %param.20) | copy-start | bytes 3076
  336.9 8.8 %copy-start.3 = (bf16[256,172]{0,1:T(8,128)(2,1)S(1)}, bf16[256,172]{0,1:T(8,128)(2,1)}, u32[]{:S(2)}) copy-start(bf16[256,172]{0,1:T(8,128)(2,1)} %param.22) | copy-start | bytes 264196
  336.9 8.8 %copy-start.7 = (f32[172]{0:T(256)S(1)}, f32[172]{0:T(256)}, u32[]{:S(2)}) copy-start(f32[172]{0:T(256)} %param.23) | copy-start | bytes 2068
  336.9 9.3 %copy-start.8 = (s32[64]{0:T(128)S(1)}, s32[64]{0:T(128)}, u32[]{:S(2)}) copy-start(s32[64]{0:T(128)} %param.17) | copy-start | bytes 772
  353.2 2.3 copy-start.2
Sparse Core Ops, SparseCore 0:
  164.3 44.5 all-gather.1
  357.4 129.1 all-reduce.3
where the time goes:
time: 502 us; the launch traced here: 500 us
  local copies, waits for them, and re-layouts  244 us (49%)
  waiting for transfers between devices  137 us (27%)
  blocking collectives  52.5 us (10%)
  other arithmetic  34.2 us (7%)
  between operations  14.3 us (3%)
  matrix products  12.8 us (3%)
    psum x1, waiting for transfers between devices, shards(): lax.psum((grad_self_one, grad_neigh_one, grad_bias_one, grad_self_two, gr...  90 us
    gather x1, local copies, waits for them, and re-layouts, shards(): from_far = returned[owners, jnp.maximum(slots, 0)]  76.5 us
    unnamed x29, local copies, waits for them, and re-layouts  58.4 us
    gather x1, local copies, waits for them, and re-layouts, shards(): position = partition_map[wanted]  54.9 us
    all_gather x1, waiting for transfers between devices, shards(): hub_rows = lax.all_gather(features[:HOT_DEV], 'dom', axis=0, tiled=True)  47.2 us
    psum x1, blocking collectives, shards(): lax.psum((grad_self_one, grad_neigh_one, grad_bias_one, grad_self_two, gr...  38.8 us
    gather x1, local copies, waits for them, and re-layouts, shards(): from_hub = hub_rows[owners * HOT_DEV + jnp.minimum(local_rows, HOT_DEV - 1)]  21.8 us
    gather x2, local copies, waits for them, and re-layouts, shards(): features[arrived]  13.9 us
  transfers between devices with their start and end apart: 3, of which 2 were waited for; matrix products, arithmetic and copies ran while one was open for 5% of the time, Pallas kernels for 0%

commit v1 on v0

--- a/solution.py
+++ b/solution.py
@@ -162,15 +162,18 @@
         grads
     )
     summed = lax.psum(
-        (
-            grad_self_one,
-            grad_neigh_one,
-            grad_bias_one,
-            grad_self_two,
-            grad_neigh_two,
-            grad_bias_two,
+        lax.psum(
+            (
+                grad_self_one,
+                grad_neigh_one,
+                grad_bias_one,
+                grad_self_two,
+                grad_neigh_two,
+                grad_bias_two,
+            ),
+            "dom",
         ),
-        ("dom", "rep"),
+        "rep",
     )
     return (seed_loss, summed[0], summed[1], summed[2], summed[3], summed[4], summed[5])
 

time: 502 us -> 501 us (level)
    psum x1, blocking collectives: 38.8 us -> 31.6 us  [shards(): lax.psum((grad_self_one, grad_neigh_one, grad_bias_one, grad_self_two, gr...]
    psum x0 -> x1, blocking collectives: none -> 5.47 us  [shards(): lax.psum(lax.psum((grad_self_one, grad_neigh_one, grad_bias_one, grad_sel...]
  transfers between devices with their start and end apart: 3 -> 4, of which waited for: 2 -> 2; matrix products, arithmetic and copies ran while one was open for 5% -> 5% of each run, Pallas kernels for 0% -> 0%
where the time goes in v1:
time: 501 us; the launch traced here: 499 us
  local copies, waits for them, and re-layouts  244 us (49%)
  waiting for transfers between devices  138 us (28%)
  blocking collectives  50.9 us (10%)
  other arithmetic  34.2 us (7%)
  between operations  14 us (3%)
  matrix products  12.8 us (3%)
    psum x1, waiting for transfers between devices, shards(): lax.psum((grad_self_one, grad_neigh_one, grad_bias_one, grad_self_two, gr...  91 us
    gather x1, local copies, waits for them, and re-layouts, shards(): from_far = returned[owners, jnp.maximum(slots, 0)]  76.5 us
    unnamed x29, local copies, waits for them, and re-layouts  58.4 us
    gather x1, local copies, waits for them, and re-layouts, shards(): position = partition_map[wanted]  54.9 us
    all_gather x1, waiting for transfers between devices, shards(): hub_rows = lax.all_gather(features[:HOT_DEV], 'dom', axis=0, tiled=True)  47.2 us
    psum x1, blocking collectives, shards(): lax.psum((grad_self_one, grad_neigh_one, grad_bias_one, grad_self_two, gr...  31.6 us
    gather x1, local copies, waits for them, and re-layouts, shards(): from_hub = hub_rows[owners * HOT_DEV + jnp.minimum(local_rows, HOT_DEV - 1)]  21.8 us
    gather x2, local copies, waits for them, and re-layouts, shards(): features[arrived]  13.9 us
  transfers between devices with their start and end apart: 4, of which 2 were waited for; matrix products, arithmetic and copies ran while one was open for 5% of the time, Pallas kernels for 0%

profile of v1, /device:TPU:0, one launch (start us, length us, event | category | flops | bytes accessed | tf_op | source)
XLA Modules:
  0.0 498.9 jit_solution(10463376944205172009)
XLA Ops:
  7.2 1.2 copy.25
  8.7 0.8 copy.24
  9.7 0.8 concatenate.37
  10.6 54.9 %gather_fusion = s32[10624]{0:T(1024)S(1)} fusion(s32[131072]{0:T(1024)S(1)} %copy-done, s32[11264]{0:T(1024)S(1)} %pad_clamp_fusion.1), kind=kCustom, calls=%fused_computation | custom fusion | bytes 127488 | tf_op jit(solution)/shard_map/gather | solution.py:132
  65.6 0.9 fusion.11
  66.6 9.2 %reduce-window.6 = s32[16,83,128]{2,1,0:T(8,128)S(1)} reduce-window(s32[16,83,128]{2,1,0:T(8,128)} %fusion.11, s32[]{:T(128)} %constant.33.clone.1), window={size=1x1x128 pad=0_0x0_0x127_0}, to_apply=%region_0.1 | reduce-window | flops 21587968 | bytes 1359876 | tf_op jit(solution)/shard_map/reduce-window
  75.8 0.6 slice_reduce_fusion
  77.1 0.8 or_reduce_fusion
  78.3 50.0 %scatter_custom_fusion = s32[5312]{0:T(1024)S(1)} fusion(s32[10624]{0:T(1024)S(1)} %broadcast_select_fusion.1, s32[10624]{0:T(1024)S(1)} %get-tuple-element.28, s32[]{:T(128)} %constant.33.clone.1), kind=kCustom, calls=%fused_computation.111 | custom fusion | bytes 21252
  128.4 13.8 %all_to_all.17 = s32[16,1,332]{2,1,0:T(1,128)S(1)} all-to-all(s32[16,1,332]{2,1,0:T(1,128)S(1)} %all_to_all.11), channel_id=1, replica_groups=mesh['dom'=16,'rep'=2] {'dom'}, dimensions={0} | all-to-all | bytes 42496 | tf_op jit(solution)/shard_map/all_to_all | solution.py:138
  142.4 11.6 %gather_fusion.1 = bf16[5312,128]{1,0:T(8,128)(2,1)} fusion(bf16[8192,128]{1,0:T(8,128)(2,1)S(1)} %copy-done.1, s32[6144]{0:T(1024)S(1)} %pad_clamp_fusion.2), kind=kCustom, calls=%fused_computation.1 | custom fusion | bytes 2740992 | tf_op jit(solution)/shard_map/gather | solution.py:139
  154.0 2.3 reshape.364
  156.3 4.4 all-to-all-start.1
  160.8 0.6 slice.20
  161.7 47.2 %all-gather.2.cloned.1.call-done = bf16[4096,128]{1,0:T(8,128)(2,1)} async-done(((bf16[256,128]{1,0:T(8,128)(2,1)}), bf16[4096,128]{1,0:T(8,128)(2,1)}) %all-gather.2.cloned.1.call-update) | async-done | bytes 1048592 | tf_op jit(solution)/shard_map/all_gather | solution.py:140
  208.9 21.8 %gather_fusion.3 = bf16[10624,128]{1,0:T(8,128)(2,1)} fusion(bf16[4096,128]{1,0:T(8,128)(2,1)} %all-gather.2.cloned.1.call-done, s32[11264]{0:T(1024)S(1)} %pad_clamp_fusion), kind=kCustom, calls=%fused_computation.3 | custom fusion | bytes 5481984 | tf_op jit(solution)/shard_map/gather | solution.py:142
  230.7 1.7 copy.26
  232.4 76.5 %gather_fusion.2 = bf16[10624,128]{1,0:T(8,128)(2,1)} fusion(bf16[16,332,128]{2,0,1:T(8,128)(2,1)S(1)} %copy.26, s32[10624]{0:T(1024)S(1)} %get-tuple-element.25), kind=kCustom, calls=%fused_computation.2 | custom fusion | bytes 5524480 | tf_op jit(solution)/shard_map/gather | solution.py:141
  309.0 7.6 %broadcast_select_fusion = bf16[10624,128]{1,0:T(8,128)(2,1)S(1)} fusion(bf16[10624,128]{1,0:T(8,128)(2,1)} %gather_fusion.2, bf16[10624,128]{1,0:T(8,128)(2,1)} %gather_fusion.3, pred[10624]{0:T(1024)(128)(4,1)S(1)} %get-tuple-element.27), kind=kLoop, calls=%fused_computation.5 | loop fusion | flops 1359872 | bytes 8169856 | tf_op jit(solution)/shard_map/jit(_where)/select_n | solution.py:143
  316.5 2.4 slice_convert_fusion
  318.9 0.8 slice_convert_fusion.1
  319.7 1.3 fusion.17
  321.0 0.8 fusion.39
  321.8 6.6 %reshape.353 = f32[960,10,128]{2,1,0:T(8,128)} reshape(f32[9600,128]{1,0:T(8,128)} %slice_convert_fusion) | data formatting | bytes 9830400 | tf_op jit(solution)/shard_map/convert_element_type | solution.py:32
  328.4 5.3 %reduce_sum.83 = f32[960,128]{1,0:T(8,128)} reduce(f32[960,10,128]{2,1,0:T(8,128)} %reshape.353, f32[]{:T(128)} %constant.78.clone.1), dimensions={1}, to_apply=%region_5.6 | reduce | flops 1105920 | bytes 5406724 | tf_op jit(solution)/shard_map/reduce_sum | solution.py:32
  333.7 3.2 fusion.15
  336.9 2.3 reshape.354
  339.2 1.4 reduce_sum.84
  340.7 1.9 reshape.352
  342.5 1.1 reduce_sum.82
  343.6 1.0 fusion.2
  344.6 1.1 fusion.52
  346.5 1.1 convert_reduce_fusion.2
  347.6 0.9 fusion.41
  348.5 0.9 fusion.51
  349.8 1.1 broadcast_in_dim.13
  350.9 2.3 reshape.346
  353.2 2.3 convert_reduce_fusion
  355.4 0.9 convolution_add_fusion.1
  356.4 0.9 convolution_add_fusion.2
  357.4 91.0 %all-reduce.7.cloned.1.call-done = (f32[128,256]{1,0:T(8,128)}, f32[128,256]{1,0:T(8,128)}, f32[256,172]{0,1:T(8,128)}, f32[256,172]{0,1:T(8,128)}) async-done(((f32[128,256]{1,0:T(8,128)}, f32[128,256]{1,0:T(8,128)}, f32[256,172]{0,1:T(8,128)}, f32[256,172]{0,1:T(8,128)}), (f32[128,256]{1,0:T(8,128)}, f32[128,256]{1,0:T(8,128)}, f32[256,172]{0,1:T(8,128)}, ...) | async-done | bytes 614416 | tf_op jit(solution)/shard_map/psum | solution.py:165
  448.4 0.5 neg.3
  448.9 31.6 %all-reduce = (f32[256]{0:T(256)S(1)}, f32[172]{0:T(256)S(1)}) all-reduce(f32[256]{0:T(256)S(1)} %add.228, f32[172]{0:T(256)S(1)} %get-tuple-element.19), channel_id=1, replica_groups=mesh['dom'=16,'rep'=2] {'dom'}, use_global_device_ids=true, to_apply=%region_16.17 | all-reduce | flops 428 | bytes 3424 | tf_op jit(solution)/shard_map/psum | solution.py:165
  480.5 5.5 %all-reduce.2 = (f32[256]{0:T(256)}, f32[172]{0:T(256)}) all-reduce(f32[256]{0:T(256)S(1)} %get-tuple-element.7, f32[172]{0:T(256)S(1)} %get-tuple-element.8), channel_id=1, replica_groups=mesh['dom'=16,'rep'=2] {'rep'}, use_global_device_ids=true, to_apply=%region_17.18 | all-reduce | flops 428 | bytes 3424 | tf_op jit(solution)/shard_map/psum | solution.py:164
  486.0 1.6 copy.37
  487.6 1.6 copy.38
  489.1 1.6 copy.39
  490.7 1.6 copy.40
  (58 shorter events, 3.8 us)
Async XLA Ops:
  7.2 3.4 copy-start
  65.6 12.3 %copy-start.10 = (s32[2]{0:T(128)S(1)}, s32[2]{0:T(128)}, u32[]{:S(2)}) copy-start(s32[2]{0:T(128)} %constant.89) | copy-start | bytes 28
  65.6 12.5 %copy-start.9 = (s32[2]{0:T(128)S(1)}, s32[2]{0:T(128)}, u32[]{:S(2)}) copy-start(s32[2]{0:T(128)} %constant.92) | copy-start | bytes 28
  66.6 75.8 %copy-start.1 = (bf16[8192,128]{1,0:T(8,128)(2,1)S(1)}, bf16[8192,128]{1,0:T(8,128)(2,1)}, u32[]{:S(2)}) copy-start(bf16[8192,128]{1,0:T(8,128)(2,1)} %param.12) | copy-start | bytes 6291460
  156.3 74.4 %all-to-all-start.1 = ((bf16[16,332,128]{2,1,0:T(8,128)(2,1)}), bf16[16,332,128]{2,1,0:T(8,128)(2,1)}, u32[]{:S(2)}, u32[]{:S(2)}) async-start(bf16[16,332,128]{2,1,0:T(8,128)(2,1)} %reshape.364), calls=%async_computation.1 | async-start | bytes 2752512 | tf_op jit(solution)/shard_map/all_to_all | solution.py:139
  160.7 48.2 %all-gather.2.cloned.1.call-start = ((), (), s32[]{:S(2)}) async-start(), calls=%async_computation.2 | async-start | bytes 1114112 | tf_op jit(solution)/shard_map/all_gather | solution.py:140
  161.5 286.9 %all-reduce.7.cloned.1.call-start = ((), (), s32[]{:S(2)}) async-start(), calls=%async_computation.3 | async-start | bytes 1245184 | tf_op jit(solution)/shard_map/psum | solution.py:165
  316.5 3.2 copy-start.5
  328.4 5.3 %copy-start.4 = (bf16[128,256]{1,0:T(8,128)(2,1)S(1)}, bf16[128,256]{1,0:T(8,128)(2,1)}, u32[]{:S(2)}) copy-start(bf16[128,256]{1,0:T(8,128)(2,1)} %param.19) | copy-start | bytes 196612
  328.4 5.3 %copy-start.6 = (f32[256]{0:T(256)S(1)}, f32[256]{0:T(256)}, u32[]{:S(2)}) copy-start(f32[256]{0:T(256)} %param.20) | copy-start | bytes 3076
  336.9 8.8 %copy-start.3 = (bf16[256,172]{0,1:T(8,128)(2,1)S(1)}, bf16[256,172]{0,1:T(8,128)(2,1)}, u32[]{:S(2)}) copy-start(bf16[256,172]{0,1:T(8,128)(2,1)} %param.22) | copy-start | bytes 264196
  336.9 8.8 %copy-start.7 = (f32[172]{0:T(256)S(1)}, f32[172]{0:T(256)}, u32[]{:S(2)}) copy-start(f32[172]{0:T(256)} %param.23) | copy-start | bytes 2068
  336.9 9.3 %copy-start.8 = (s32[64]{0:T(128)S(1)}, s32[64]{0:T(128)}, u32[]{:S(2)}) copy-start(s32[64]{0:T(128)} %param.17) | copy-start | bytes 772
  353.2 2.3 copy-start.2
  357.3 128.7 %all-reduce.9.cloned.1.call-start = ((), (), s32[]{:S(2)}) async-start(), calls=%async_computation.4 | async-start | bytes 1245184 | tf_op jit(solution)/shard_map/psum | solution.py:164
Sparse Core Ops, SparseCore 0:
  164.3 44.5 all-gather.1
  357.4 90.8 all-reduce.6
  450.8 31.0 all-reduce.8
